TPU v7x, 32 devices: a whole 2x2x4 slice. The times are simulated.
32 devices in a mesh: rows: 8 (over y, x, core), feat: 4 (over z).
Axes of the slice: x: 2, y: 2, z: 4, core: 2. Of those that a mesh axis runs over, the one named last changes fastest.
Arguments:
- bins: int32 [8192, 512], P('rows', 'feat'), may hold values from -2147483648 to 2147483647, as said below
- hessian: float32 [32768], P('rows'), may hold values from 0.05 to 1
- thresholds: float32 [128], replicated, may hold values from 0.02 to 0.98
Outputs:
- cuts: float32 [512, 128], P('feat')
Inputs may be any that keep to these rules, and one draw needn't show every extreme that they name: `bins`: each word holds the bin ids, 0 to 255, of rows 4i to 4i + 3 of one feature, row 4i + k in bits 8k to 8k + 7 of the two's complement word.
All inputs are finite; a program needn't handle non-finite values.
Results may differ from a plain program's by a relative error of at most 0.000065.
Values sent between devices are 32-bit elements; how exact they have to be, the bound alone decides.
A program may use at most 192 MiB of HBM per device.

v0:
```python
import math
import jax
import jax.numpy as jnp
from jax import lax
from jax.sharding import PartitionSpec as P

BINS = 256


def unpack(words):
    parts = [jnp.bitwise_and(jnp.right_shift(words, 8 * k), 255) for k in range(4)]
    stacked = jnp.stack(parts, axis=1)
    return stacked.reshape(words.shape[0] * 4, words.shape[1])


def histogram(columns, weights):
    count, width = columns.shape
    limit = max(8, 1048576 // (width * 16))
    block = math.gcd(count, limit)
    col_blocks = columns.reshape(count // block, block, width)
    wt_blocks = weights.reshape(count // block, block)
    levels = jnp.arange(16, dtype=jnp.int32)

    def add_block(total, item):
        col_part, wt_part = item
        high = jnp.right_shift(col_part, 4)
        low = jnp.bitwise_and(col_part, 15)
        high_hot = jnp.where(high[:, :, None] == levels, wt_part[:, None, None], 0.0)
        low_hot = (low[:, :, None] == levels).astype(jnp.float32)
        joint = jnp.einsum("rkh,rkl->khl", high_hot, low_hot, precision=lax.Precision.HIGHEST)
        return (total + joint, None)

    start = jnp.zeros((width, 16, 16), jnp.float32)
    total, unused = lax.scan(add_block, start, (col_blocks, wt_blocks))
    return total.reshape(width, BINS)


def cut_positions(hist, thresholds):
    cum = jnp.cumsum(hist, axis=1)
    before = cum - hist
    total = cum[:, -1]
    target = thresholds[None, :, None] * total[:, None, None]
    ratio = (target - before[:, None, :]) / (hist[:, None, :] + 1.0)
    return jnp.sum(jnp.clip(ratio, 0.0, 1.0), axis=2)


def local(bins, hessian, thresholds):
    regrouped = lax.all_to_all(bins, "rows", split_axis=1, concat_axis=0, tiled=True)
    weights = lax.all_gather(hessian, "rows", axis=0, tiled=True)
    hist = histogram(unpack(regrouped), weights)
    cuts = cut_positions(hist, thresholds)
    return lax.all_gather(cuts, "rows", axis=0, tiled=True)


def solution(mesh):
    in_specs = (P("rows", "feat"), P("rows"), P())
    out_specs = P("feat", None)
    return jax.shard_map(local, mesh=mesh, in_specs=in_specs, out_specs=out_specs, check_vma=False)
```

profile of v0, /device:TPU:0, one launch (start us, length us, event | category | flops | bytes accessed | tf_op | source)
XLA Modules:
  0.0 84.6 jit_solution(17974510913110473244)
XLA Ops:
  0.0 2.0 %copy.34 = s32[1024,128]{0,1:T(8,128)} copy(s32[1024,128]{1,0:T(8,128)} %param.5) | data formatting | bytes 1048576 | tf_op args[0]
  2.0 5.2 %all-to-all-start = ((s32[1024,8,16]{0,2,1:T(8,128)}), s32[1024,8,16]{0,2,1:T(8,128)S(1)}, u32[]{:S(2)}, u32[]{:S(2)}) async-start(s32[1024,8,16]{0,2,1:T(8,128)} %bitcast), calls=%async_computation | async-start | bytes 1048576 | tf_op jit(solution)/shard_map/all_to_all | solution.py:48
  7.3 13.2 %all_gather.6 = f32[32768]{0:T(1024)S(1)} all-gather(f32[4096]{0:T(1024)S(1)} %copy-done), channel_id=1, replica_groups=mesh['rows'=8,'feat'=4] {'rows'}, dimensions={0}, use_global_device_ids=true | all-gather | bytes 147456 | tf_op jit(solution)/shard_map/all_gather | solution.py:49
  20.7 0.3 copy.35
  21.2 0.3 copy.36
  21.6 0.3 copy.37
  21.9 0.9 %and.82 = s32[8192,1,16]{0,2,1:T(8,128)} reshape(s32[8,1024,16]{1,0,2:T(8,128)S(1)} %copy.37) | data formatting | bytes 1048576 | tf_op jit(solution)/shard_map/and | solution.py:11
  23.1 0.9 %and.85 = s32[8192,1,16]{0,2,1:T(8,128)} reshape(s32[8,1024,16]{1,0,2:T(8,128)S(1)} %copy.38) | data formatting | bytes 1048576 | tf_op jit(solution)/shard_map/and | solution.py:11
  24.0 1.3 %pad_add_fusion = s32[8192,4,16]{0,2,1:T(8,128)S(1)} fusion(s32[8192,1,16]{0,2,1:T(8,128)} %and.85, s32[8192,1,16]{0,2,1:T(8,128)} %and.82, s32[8192,1,16]{0,2,1:T(8,128)S(1)} %and.79, s32[8192,1,16]{0,2,1:T(8,128)S(1)} %and.76), kind=kLoop, calls=%fused_computation.14 | loop fusion | flops 1572864 | bytes 4194304 | tf_op jit(solution)/shard_map/stack | solution.py:12
  25.4 10.7 %copy.39 = s32[8192,4,16]{2,1,0:T(4,128)} copy(s32[8192,4,16]{0,2,1:T(8,128)S(1)} %pad_add_fusion) | data formatting | bytes 4194304 | tf_op jit(solution)/shard_map/stack | solution.py:12
  36.1 9.6 %copy.40 = s32[8,4096,16]{1,2,0:T(8,128)S(1)} copy(s32[8,4096,16]{2,1,0:T(8,128)} %bitcast.35) | data formatting | bytes 4194304
  45.7 27.9 %while.12 = (s32[]{:T(128)}, f32[16,16,16]{2,1,0:T(8,128)S(1)}, s32[8,4096,16]{1,2,0:T(8,128)S(1)}, f32[8,4096]{1,0:T(8,128)S(1)}, s32[]{:T(128)}, /*index=5*/s32[]{:T(128)}) while((s32[]{:T(128)}, f32[16,16,16]{2,1,0:T(8,128)S(1)}, s32[8,4096,16]{1,2,0:T(8,128)S(1)}, f32[8,4096]{1,0:T(8,128)S(1)}, s32[]{:T(128)}, ...), condition=%wide.region_1.2_spmd.clone.clone, body=%wide.region_0.1_spmd.clone.clone.sunk | while | flops 204611584 | bytes 1392727 | solution.py:34
  45.8 3.4 %fusion.16 = f32[16,16,16]{2,1,0:T(8,128)S(1)} fusion(s32[4096,16]{0,1:T(8,128)S(1)} %get-tuple-element.126, f32[4096]{0:T(1024)S(1)} %bitcast.36, s32[4096,16]{0,1:T(8,128)S(1)} %get-tuple-element.127, f32[16,16,16]{2,1,0:T(8,128)S(1)} %get-tuple-element.135, pred[]{:T(512)S(6)} %compare.3), kind=kOutput, calls=%fused_computation.9.clone.1 | convolution fusion | flops 204480512 | bytes 573441 | tf_op jit(solution)/shard_map/while/body/eval_jaxpr/rkh,rkl->khl/dot_general | solution.py:30
  49.3 3.4 %fusion.16 = f32[16,16,16]{2,1,0:T(8,128)S(1)} fusion(s32[4096,16]{0,1:T(8,128)S(1)} %get-tuple-element.126, f32[4096]{0:T(1024)S(1)} %bitcast.36, s32[4096,16]{0,1:T(8,128)S(1)} %get-tuple-element.127, f32[16,16,16]{2,1,0:T(8,128)S(1)} %get-tuple-element.135, pred[]{:T(512)S(6)} %compare.3), kind=kOutput, calls=%fused_computation.9.clone.1 | convolution fusion | flops 204480512 | bytes 573441 | tf_op jit(solution)/shard_map/while/body/eval_jaxpr/rkh,rkl->khl/dot_general | solution.py:30
  52.8 3.4 %fusion.16 = f32[16,16,16]{2,1,0:T(8,128)S(1)} fusion(s32[4096,16]{0,1:T(8,128)S(1)} %get-tuple-element.126, f32[4096]{0:T(1024)S(1)} %bitcast.36, s32[4096,16]{0,1:T(8,128)S(1)} %get-tuple-element.127, f32[16,16,16]{2,1,0:T(8,128)S(1)} %get-tuple-element.135, pred[]{:T(512)S(6)} %compare.3), kind=kOutput, calls=%fused_computation.9.clone.1 | convolution fusion | flops 204480512 | bytes 573441 | tf_op jit(solution)/shard_map/while/body/eval_jaxpr/rkh,rkl->khl/dot_general | solution.py:30
  56.2 3.4 %fusion.16 = f32[16,16,16]{2,1,0:T(8,128)S(1)} fusion(s32[4096,16]{0,1:T(8,128)S(1)} %get-tuple-element.126, f32[4096]{0:T(1024)S(1)} %bitcast.36, s32[4096,16]{0,1:T(8,128)S(1)} %get-tuple-element.127, f32[16,16,16]{2,1,0:T(8,128)S(1)} %get-tuple-element.135, pred[]{:T(512)S(6)} %compare.3), kind=kOutput, calls=%fused_computation.9.clone.1 | convolution fusion | flops 204480512 | bytes 573441 | tf_op jit(solution)/shard_map/while/body/eval_jaxpr/rkh,rkl->khl/dot_general | solution.py:30
  59.7 3.4 %fusion.16 = f32[16,16,16]{2,1,0:T(8,128)S(1)} fusion(s32[4096,16]{0,1:T(8,128)S(1)} %get-tuple-element.126, f32[4096]{0:T(1024)S(1)} %bitcast.36, s32[4096,16]{0,1:T(8,128)S(1)} %get-tuple-element.127, f32[16,16,16]{2,1,0:T(8,128)S(1)} %get-tuple-element.135, pred[]{:T(512)S(6)} %compare.3), kind=kOutput, calls=%fused_computation.9.clone.1 | convolution fusion | flops 204480512 | bytes 573441 | tf_op jit(solution)/shard_map/while/body/eval_jaxpr/rkh,rkl->khl/dot_general | solution.py:30
  63.2 3.4 %fusion.16 = f32[16,16,16]{2,1,0:T(8,128)S(1)} fusion(s32[4096,16]{0,1:T(8,128)S(1)} %get-tuple-element.126, f32[4096]{0:T(1024)S(1)} %bitcast.36, s32[4096,16]{0,1:T(8,128)S(1)} %get-tuple-element.127, f32[16,16,16]{2,1,0:T(8,128)S(1)} %get-tuple-element.135, pred[]{:T(512)S(6)} %compare.3), kind=kOutput, calls=%fused_computation.9.clone.1 | convolution fusion | flops 204480512 | bytes 573441 | tf_op jit(solution)/shard_map/while/body/eval_jaxpr/rkh,rkl->khl/dot_general | solution.py:30
  66.7 3.4 %fusion.16 = f32[16,16,16]{2,1,0:T(8,128)S(1)} fusion(s32[4096,16]{0,1:T(8,128)S(1)} %get-tuple-element.126, f32[4096]{0:T(1024)S(1)} %bitcast.36, s32[4096,16]{0,1:T(8,128)S(1)} %get-tuple-element.127, f32[16,16,16]{2,1,0:T(8,128)S(1)} %get-tuple-element.135, pred[]{:T(512)S(6)} %compare.3), kind=kOutput, calls=%fused_computation.9.clone.1 | convolution fusion | flops 204480512 | bytes 573441 | tf_op jit(solution)/shard_map/while/body/eval_jaxpr/rkh,rkl->khl/dot_general | solution.py:30
  70.2 3.4 %fusion.16 = f32[16,16,16]{2,1,0:T(8,128)S(1)} fusion(s32[4096,16]{0,1:T(8,128)S(1)} %get-tuple-element.126, f32[4096]{0:T(1024)S(1)} %bitcast.36, s32[4096,16]{0,1:T(8,128)S(1)} %get-tuple-element.127, f32[16,16,16]{2,1,0:T(8,128)S(1)} %get-tuple-element.135, pred[]{:T(512)S(6)} %compare.3), kind=kOutput, calls=%fused_computation.9.clone.1 | convolution fusion | flops 204480512 | bytes 573441 | tf_op jit(solution)/shard_map/while/body/eval_jaxpr/rkh,rkl->khl/dot_general | solution.py:30
  73.8 0.6 reduce-window.6
  75.0 0.7 clamp_reduce_fusion
  75.7 8.3 %all_gather.7 = f32[128,128]{1,0:T(8,128)S(1)} all-gather(f32[16,128]{1,0:T(8,128)S(1)} %clamp_reduce_fusion), channel_id=1, replica_groups=mesh['rows'=8,'feat'=4] {'rows'}, dimensions={0}, use_global_device_ids=true | all-gather | bytes 73728 | tf_op jit(solution)/shard_map/all_gather | solution.py:52
  84.0 0.6 copy.54
  (37 shorter events, 2.1 us)
Async XLA Ops:
  0.0 7.2 %copy-start = (f32[4096]{0:T(1024)S(1)}, f32[4096]{0:T(1024)}, u32[]{:S(2)}) copy-start(f32[4096]{0:T(1024)} %param.6) | copy-start | bytes 49156
  2.0 18.4 %all-to-all-start = ((s32[1024,8,16]{0,2,1:T(8,128)}), s32[1024,8,16]{0,2,1:T(8,128)S(1)}, u32[]{:S(2)}, u32[]{:S(2)}) async-start(s32[1024,8,16]{0,2,1:T(8,128)} %bitcast), calls=%async_computation | async-start | bytes 1048576 | tf_op jit(solution)/shard_map/all_to_all | solution.py:48
  45.7 29.3 %copy-start.1 = (f32[128]{0:T(128)S(1)}, f32[128]{0:T(128)}, u32[]{:S(2)}) copy-start(f32[128]{0:T(128)} %param.7) | copy-start | bytes 1540
where the time goes:
time: 85 us; the launch traced here: 84.6 us
  matrix products  27.1 us (32%)
  local copies, waits for them, and re-layouts  27 us (32%)
  blocking collectives  21.5 us (25%)
  starting transfers between devices  5.2 us (6%)
  other arithmetic  3.46 us (4%)
    dot_general x8, matrix products, add_block(): jnp.einsum('rkh,rkl->khl', high_hot, low_hot, precision=lax.Precision.HIG...  27.1 us
    all_gather x1, blocking collectives, local(): weights = lax.all_gather(hessian, 'rows', axis=0, tiled=True)  13.2 us
    unnamed x7, local copies, waits for them, and re-layouts  12.3 us
    another operation x1, local copies, waits for them, and re-layouts, unpack(): stacked = jnp.stack(parts, axis=1)  10.7 us
    all_gather x1, blocking collectives, local(): return lax.all_gather(cuts, 'rows', axis=0, tiled=True)  8.29 us
    all_to_all x1, starting transfers between devices, local(): lax.all_to_all(bins, 'rows', split_axis=1, concat_axis=0, tiled=True)  5.2 us
    and x8, local copies, waits for them, and re-layouts, unpack(): jnp.bitwise_and(jnp.right_shift(words, 8 * k), 255)  3.23 us
  transfers between devices with their start and end apart: 1, of which 0 were waited for; matrix products, arithmetic and copies ran while one was open for 0% of the time, Pallas kernels for 0%

commit v1 on v0

--- a/solution.py
+++ b/solution.py
@@ -49,7 +49,9 @@
     weights = lax.all_gather(hessian, "rows", axis=0, tiled=True)
     hist = histogram(unpack(regrouped), weights)
     cuts = cut_positions(hist, thresholds)
-    return lax.all_gather(cuts, "rows", axis=0, tiled=True)
+    return jnp.concatenate(
+        lax.all_to_all(jnp.stack([cuts] * lax.axis_size("rows")), "rows", 0, 0), axis=0
+    )
 
 
 def solution(mesh):

time: 85 us -> 84.3 us (level)
    all_gather x1 -> x0, blocking collectives: 8.29 us -> none  [local(): return lax.all_gather(cuts, 'rows', axis=0, tiled=True)]
    all_to_all x0 -> x1, blocking collectives: none -> 7.54 us  [local(): lax.all_to_all(jnp.stack([cuts] * lax.axis_size('rows')), 'rows', 0, 0)]
where the time goes in v1:
time: 84.3 us; the launch traced here: 83.9 us
  matrix products  27.1 us (32%)
  local copies, waits for them, and re-layouts  27 us (32%)
  blocking collectives  20.7 us (25%)
  starting transfers between devices  5.2 us (6%)
  other arithmetic  3.46 us (4%)
    dot_general x8, matrix products, add_block(): jnp.einsum('rkh,rkl->khl', high_hot, low_hot, precision=lax.Precision.HIG...  27.1 us
    all_gather x1, blocking collectives, local(): weights = lax.all_gather(hessian, 'rows', axis=0, tiled=True)  13.2 us
    unnamed x7, local copies, waits for them, and re-layouts  12.3 us
    another operation x1, local copies, waits for them, and re-layouts, unpack(): stacked = jnp.stack(parts, axis=1)  10.7 us
    all_to_all x1, blocking collectives, local(): lax.all_to_all(jnp.stack([cuts] * lax.axis_size('rows')), 'rows', 0, 0)  7.54 us
    all_to_all x1, starting transfers between devices, local(): lax.all_to_all(bins, 'rows', split_axis=1, concat_axis=0, tiled=True)  5.2 us
    and x8, local copies, waits for them, and re-layouts, unpack(): jnp.bitwise_and(jnp.right_shift(words, 8 * k), 255)  3.23 us
  transfers between devices with their start and end apart: 1, of which 0 were waited for; matrix products, arithmetic and copies ran while one was open for 0% of the time, Pallas kernels for 0%

profile of v1, /device:TPU:0, one launch (start us, length us, event | category | flops | bytes accessed | tf_op | source)
XLA Modules:
  0.0 83.9 jit_solution(6978148942795891849)
XLA Ops:
  0.0 2.0 %copy.34 = s32[1024,128]{0,1:T(8,128)} copy(s32[1024,128]{1,0:T(8,128)} %param.5) | data formatting | bytes 1048576 | tf_op args[0]
  2.0 5.2 %all-to-all-start = ((s32[1024,8,16]{0,2,1:T(8,128)}), s32[1024,8,16]{0,2,1:T(8,128)S(1)}, u32[]{:S(2)}, u32[]{:S(2)}) async-start(s32[1024,8,16]{0,2,1:T(8,128)} %bitcast), calls=%async_computation | async-start | bytes 1048576 | tf_op jit(solution)/shard_map/all_to_all | solution.py:48
  7.3 13.2 %all_gather.3 = f32[32768]{0:T(1024)S(1)} all-gather(f32[4096]{0:T(1024)S(1)} %copy-done), channel_id=1, replica_groups=mesh['rows'=8,'feat'=4] {'rows'}, dimensions={0}, use_global_device_ids=true | all-gather | bytes 147456 | tf_op jit(solution)/shard_map/all_gather | solution.py:49
  20.7 0.3 copy.35
  21.2 0.3 copy.36
  21.6 0.3 copy.37
  21.9 0.9 %and.82 = s32[8192,1,16]{0,2,1:T(8,128)} reshape(s32[8,1024,16]{1,0,2:T(8,128)S(1)} %copy.37) | data formatting | bytes 1048576 | tf_op jit(solution)/shard_map/and | solution.py:11
  23.1 0.9 %and.85 = s32[8192,1,16]{0,2,1:T(8,128)} reshape(s32[8,1024,16]{1,0,2:T(8,128)S(1)} %copy.38) | data formatting | bytes 1048576 | tf_op jit(solution)/shard_map/and | solution.py:11
  24.0 1.3 %pad_add_fusion = s32[8192,4,16]{0,2,1:T(8,128)S(1)} fusion(s32[8192,1,16]{0,2,1:T(8,128)} %and.85, s32[8192,1,16]{0,2,1:T(8,128)} %and.82, s32[8192,1,16]{0,2,1:T(8,128)S(1)} %and.79, s32[8192,1,16]{0,2,1:T(8,128)S(1)} %and.76), kind=kLoop, calls=%fused_computation.14 | loop fusion | flops 1572864 | bytes 4194304 | tf_op jit(solution)/shard_map/stack | solution.py:12
  25.4 10.7 %copy.39 = s32[8192,4,16]{2,1,0:T(4,128)} copy(s32[8192,4,16]{0,2,1:T(8,128)S(1)} %pad_add_fusion) | data formatting | bytes 4194304 | tf_op jit(solution)/shard_map/stack | solution.py:12
  36.1 9.6 %copy.40 = s32[8,4096,16]{1,2,0:T(8,128)S(1)} copy(s32[8,4096,16]{2,1,0:T(8,128)} %bitcast.36) | data formatting | bytes 4194304
  45.7 27.9 %while.12 = (s32[]{:T(128)}, f32[16,16,16]{2,1,0:T(8,128)S(1)}, s32[8,4096,16]{1,2,0:T(8,128)S(1)}, f32[8,4096]{1,0:T(8,128)S(1)}, s32[]{:T(128)}, /*index=5*/s32[]{:T(128)}) while((s32[]{:T(128)}, f32[16,16,16]{2,1,0:T(8,128)S(1)}, s32[8,4096,16]{1,2,0:T(8,128)S(1)}, f32[8,4096]{1,0:T(8,128)S(1)}, s32[]{:T(128)}, ...), condition=%wide.region_1.2_spmd.clone.clone, body=%wide.region_0.1_spmd.clone.clone.sunk | while | flops 204611584 | bytes 1392727 | solution.py:34
  45.8 3.4 %fusion.16 = f32[16,16,16]{2,1,0:T(8,128)S(1)} fusion(s32[4096,16]{0,1:T(8,128)S(1)} %get-tuple-element.126, f32[4096]{0:T(1024)S(1)} %bitcast.37, s32[4096,16]{0,1:T(8,128)S(1)} %get-tuple-element.127, f32[16,16,16]{2,1,0:T(8,128)S(1)} %get-tuple-element.135, pred[]{:T(512)S(6)} %compare.3), kind=kOutput, calls=%fused_computation.9.clone.1 | convolution fusion | flops 204480512 | bytes 573441 | tf_op jit(solution)/shard_map/while/body/eval_jaxpr/rkh,rkl->khl/dot_general | solution.py:30
  49.3 3.4 %fusion.16 = f32[16,16,16]{2,1,0:T(8,128)S(1)} fusion(s32[4096,16]{0,1:T(8,128)S(1)} %get-tuple-element.126, f32[4096]{0:T(1024)S(1)} %bitcast.37, s32[4096,16]{0,1:T(8,128)S(1)} %get-tuple-element.127, f32[16,16,16]{2,1,0:T(8,128)S(1)} %get-tuple-element.135, pred[]{:T(512)S(6)} %compare.3), kind=kOutput, calls=%fused_computation.9.clone.1 | convolution fusion | flops 204480512 | bytes 573441 | tf_op jit(solution)/shard_map/while/body/eval_jaxpr/rkh,rkl->khl/dot_general | solution.py:30
  52.8 3.4 %fusion.16 = f32[16,16,16]{2,1,0:T(8,128)S(1)} fusion(s32[4096,16]{0,1:T(8,128)S(1)} %get-tuple-element.126, f32[4096]{0:T(1024)S(1)} %bitcast.37, s32[4096,16]{0,1:T(8,128)S(1)} %get-tuple-element.127, f32[16,16,16]{2,1,0:T(8,128)S(1)} %get-tuple-element.135, pred[]{:T(512)S(6)} %compare.3), kind=kOutput, calls=%fused_computation.9.clone.1 | convolution fusion | flops 204480512 | bytes 573441 | tf_op jit(solution)/shard_map/while/body/eval_jaxpr/rkh,rkl->khl/dot_general | solution.py:30
  56.2 3.4 %fusion.16 = f32[16,16,16]{2,1,0:T(8,128)S(1)} fusion(s32[4096,16]{0,1:T(8,128)S(1)} %get-tuple-element.126, f32[4096]{0:T(1024)S(1)} %bitcast.37, s32[4096,16]{0,1:T(8,128)S(1)} %get-tuple-element.127, f32[16,16,16]{2,1,0:T(8,128)S(1)} %get-tuple-element.135, pred[]{:T(512)S(6)} %compare.3), kind=kOutput, calls=%fused_computation.9.clone.1 | convolution fusion | flops 204480512 | bytes 573441 | tf_op jit(solution)/shard_map/while/body/eval_jaxpr/rkh,rkl->khl/dot_general | solution.py:30
  59.7 3.4 %fusion.16 = f32[16,16,16]{2,1,0:T(8,128)S(1)} fusion(s32[4096,16]{0,1:T(8,128)S(1)} %get-tuple-element.126, f32[4096]{0:T(1024)S(1)} %bitcast.37, s32[4096,16]{0,1:T(8,128)S(1)} %get-tuple-element.127, f32[16,16,16]{2,1,0:T(8,128)S(1)} %get-tuple-element.135, pred[]{:T(512)S(6)} %compare.3), kind=kOutput, calls=%fused_computation.9.clone.1 | convolution fusion | flops 204480512 | bytes 573441 | tf_op jit(solution)/shard_map/while/body/eval_jaxpr/rkh,rkl->khl/dot_general | solution.py:30
  63.2 3.4 %fusion.16 = f32[16,16,16]{2,1,0:T(8,128)S(1)} fusion(s32[4096,16]{0,1:T(8,128)S(1)} %get-tuple-element.126, f32[4096]{0:T(1024)S(1)} %bitcast.37, s32[4096,16]{0,1:T(8,128)S(1)} %get-tuple-element.127, f32[16,16,16]{2,1,0:T(8,128)S(1)} %get-tuple-element.135, pred[]{:T(512)S(6)} %compare.3), kind=kOutput, calls=%fused_computation.9.clone.1 | convolution fusion | flops 204480512 | bytes 573441 | tf_op jit(solution)/shard_map/while/body/eval_jaxpr/rkh,rkl->khl/dot_general | solution.py:30
  66.7 3.4 %fusion.16 = f32[16,16,16]{2,1,0:T(8,128)S(1)} fusion(s32[4096,16]{0,1:T(8,128)S(1)} %get-tuple-element.126, f32[4096]{0:T(1024)S(1)} %bitcast.37, s32[4096,16]{0,1:T(8,128)S(1)} %get-tuple-element.127, f32[16,16,16]{2,1,0:T(8,128)S(1)} %get-tuple-element.135, pred[]{:T(512)S(6)} %compare.3), kind=kOutput, calls=%fused_computation.9.clone.1 | convolution fusion | flops 204480512 | bytes 573441 | tf_op jit(solution)/shard_map/while/body/eval_jaxpr/rkh,rkl->khl/dot_general | solution.py:30
  70.2 3.4 %fusion.16 = f32[16,16,16]{2,1,0:T(8,128)S(1)} fusion(s32[4096,16]{0,1:T(8,128)S(1)} %get-tuple-element.126, f32[4096]{0:T(1024)S(1)} %bitcast.37, s32[4096,16]{0,1:T(8,128)S(1)} %get-tuple-element.127, f32[16,16,16]{2,1,0:T(8,128)S(1)} %get-tuple-element.135, pred[]{:T(512)S(6)} %compare.3), kind=kOutput, calls=%fused_computation.9.clone.1 | convolution fusion | flops 204480512 | bytes 573441 | tf_op jit(solution)/shard_map/while/body/eval_jaxpr/rkh,rkl->khl/dot_general | solution.py:30
  73.8 0.6 reduce-window.6
  75.0 0.7 clamp_reduce_fusion
  75.7 7.5 %all_to_all.18 = f32[8,16,128]{2,1,0:T(8,128)S(1)} all-to-all(f32[8,16,128]{2,1,0:T(8,128)S(1)} %stack.5), channel_id=1, replica_groups=mesh['rows'=8,'feat'=4] {'rows'}, dimensions={0} | all-to-all | bytes 131072 | tf_op jit(solution)/shard_map/all_to_all | solution.py:53
  83.3 0.6 copy.54
  (38 shorter events, 2.1 us)
Async XLA Ops:
  0.0 7.2 %copy-start = (f32[4096]{0:T(1024)S(1)}, f32[4096]{0:T(1024)}, u32[]{:S(2)}) copy-start(f32[4096]{0:T(1024)} %param.6) | copy-start | bytes 49156
  2.0 18.4 %all-to-all-start = ((s32[1024,8,16]{0,2,1:T(8,128)}), s32[1024,8,16]{0,2,1:T(8,128)S(1)}, u32[]{:S(2)}, u32[]{:S(2)}) async-start(s32[1024,8,16]{0,2,1:T(8,128)} %bitcast), calls=%async_computation | async-start | bytes 1048576 | tf_op jit(solution)/shard_map/all_to_all | solution.py:48
  45.7 29.3 %copy-start.1 = (f32[128]{0:T(128)S(1)}, f32[128]{0:T(128)}, u32[]{:S(2)}) copy-start(f32[128]{0:T(128)} %param.7) | copy-start | bytes 1540
